TPU v7x, 32 devices: a whole 2x2x4 slice. The times are simulated.
32 devices in a mesh: dp: 16 (over z, x, core), mp: 2 (over y).
Axes of the slice: x: 2, y: 2, z: 4, core: 2. Of those that a mesh axis runs over, the one named last changes fastest.
Arguments:
- ranges: bfloat16 [512, 2652], P(('dp', 'mp')), may hold values from 0.0099487305 to 1
- board: int32 [512, 5], P(('dp', 'mp')), may hold values from 0 to 51, as said below
- targets: bfloat16 [512, 2652], P(('dp', 'mp')), may hold values from -6 to 6
- w_in: bfloat16 [1536, 2704], P(('mp', 'dp')), may hold values from -0.34570312 to 0.34570312
- w_out: bfloat16 [1536, 2652], P(('mp', 'dp')), may hold values from -0.3046875 to 0.3046875
Outputs:
- predicted: bfloat16 [512, 2652], P(('dp', 'mp'))
- update_in: float32 [1536, 2704], P(('mp', 'dp'))
- update_out: float32 [1536, 2652], P(('mp', 'dp'))
- loss: float32 [], replicated
Inputs may be any that keep to these rules, and one draw needn't show every extreme that they name: `board`: each row holds 5 different cards.
All inputs are finite; a program needn't handle non-finite values.
Results may differ from a plain program's by a relative error of at most 0.014.
Values may be sent and summed in bfloat16 or wider, within the bound.
No kernel may reach another device: no remote copies, remote signals or barrier semaphores. Data moves between devices by JAX's collectives and lax.ppermute only.
A program may use at most 64 MiB of HBM per device.

v0:
```python
import jax
import jax.numpy as jnp
from jax import lax
from jax.sharding import PartitionSpec as P

CARDS = 52
HIDDEN_SIZE = 1536


def huber_terms(error_value):
    magnitude = jnp.abs(error_value)
    return jnp.where(magnitude <= 1.0, 0.5 * error_value * error_value, magnitude - 0.5)


def build_features(all_ranges, all_board, card_count):
    card_ids = jnp.arange(card_count, dtype=jnp.int32)
    onehot_board = jnp.sum(
        (all_board[:, :, None] == card_ids[None, None, :]).astype(jnp.float32), axis=1
    ).astype(jnp.bfloat16)
    return jnp.concatenate([all_ranges, onehot_board], axis=1)


def right_product(left_side, right_block):
    return lax.dot_general(
        left_side, right_block, (((1,), (1,)), ((), ())), preferred_element_type=jnp.float32
    )


def left_product(left_side, right_side):
    return lax.dot_general(
        left_side, right_side, (((0,), (0,)), ((), ())), preferred_element_type=jnp.float32
    )


def body(ranges, board, targets, w_in, w_out):
    mp_count = lax.axis_size("mp")
    dp_count = lax.axis_size("dp")
    stored_rows = ranges.shape[0]
    value_width = w_out.shape[1]
    all_ranges, all_board = (
        lax.all_gather(ranges, "mp", axis=0, tiled=True),
        lax.all_gather(board, "mp", axis=0, tiled=True),
    )
    features = build_features(all_ranges, all_board, CARDS)
    local_in = lax.all_gather(w_in, "dp", axis=0, tiled=True)
    preact = right_product(features, local_in)
    hidden = jax.nn.gelu(preact).astype(jnp.bfloat16)
    local_out = lax.all_gather(w_out, "dp", axis=0, tiled=True)
    partial_value = jnp.dot(hidden, local_out, preferred_element_type=jnp.float32)
    stacked = partial_value.astype(jnp.bfloat16).reshape(mp_count, stored_rows, value_width)
    received = lax.all_to_all(stacked, "mp", split_axis=0, concat_axis=0, tiled=True)
    summed = jnp.sum(received.astype(jnp.float32), axis=0)
    error_value = summed - targets.astype(jnp.float32)
    own_grad = jnp.clip(error_value, -1.0, 1.0).astype(jnp.bfloat16)
    out_grad = lax.all_gather(own_grad, "mp", axis=0, tiled=True)
    predicted = summed.astype(jnp.bfloat16)
    loss_part = jnp.sum(huber_terms(error_value))
    loss_total = lax.psum(loss_part, ("dp", "mp"))
    grad_out = lax.psum_scatter(
        left_product(hidden, out_grad), "dp", scatter_dimension=0, tiled=True
    )
    back_out = lax.all_gather(w_out, "dp", axis=0, tiled=True)
    hidden_grad = right_product(out_grad, back_out)
    unused_value, gelu_back = jax.vjp(jax.nn.gelu, preact)
    preact_grad = gelu_back(hidden_grad)[0].astype(jnp.bfloat16)
    grad_in = lax.psum_scatter(
        left_product(preact_grad, features), "dp", scatter_dimension=0, tiled=True
    )
    square_part = jnp.sum(grad_in * grad_in) + jnp.sum(grad_out * grad_out)
    square_total = lax.psum(square_part, ("dp", "mp"))
    count_params = HIDDEN_SIZE * (w_in.shape[1] + value_width)
    scale = lax.rsqrt(square_total / count_params + 1e-06)
    loss = loss_total / (stored_rows * mp_count * dp_count * value_width)
    return (predicted, grad_in * scale, grad_out * scale, loss)


def solution(mesh):
    in_specs = (
        P(("dp", "mp"), None),
        P(("dp", "mp"), None),
        P(("dp", "mp"), None),
        P(("mp", "dp"), None),
        P(("mp", "dp"), None),
    )
    out_specs = (P(("dp", "mp"), None), P(("mp", "dp"), None), P(("mp", "dp"), None), P())
    return jax.shard_map(body, mesh=mesh, in_specs=in_specs, out_specs=out_specs, check_vma=False)
```

profile of v0, /device:TPU:0, one launch (start us, length us, event | category | flops | bytes accessed | tf_op | source)
XLA Modules:
  0.0 402.8 jit_solution(9901448083366208325)
XLA Ops:
  7.2 0.0 all-gather.4.cloned.1.call-start
  7.2 0.7 all-gather.4.cloned.1.call-update
  7.9 0.0 all-gather.6.cloned.1.call-start
  7.9 0.7 all-gather.6.cloned.1.call-update
  8.6 0.0 reduce-scatter.5.cloned.1.call-start
  8.7 5.5 %all-gather = s32[2,16,5]{1,2,0:T(8,128)S(1)} all-gather(s32[1,16,5]{1,2,0:T(8,128)} %bitcast.10), channel_id=1, replica_groups=mesh['dp'=16,'mp'=2] {'mp'}, dimensions={0}, use_global_device_ids=true | all-gather | bytes 960 | tf_op jit(solution)/shard_map/all_gather | solution.py:42
  14.2 0.1 reshape.14
  14.3 5.4 %all_gather.16 = bf16[32,2652]{1,0:T(8,128)(2,1)S(1)} all-gather(bf16[16,2652]{1,0:T(8,128)(2,1)} %param.5), channel_id=1, replica_groups=mesh['dp'=16,'mp'=2] {'mp'}, dimensions={0}, use_global_device_ids=true | all-gather | bytes 254592 | tf_op jit(solution)/shard_map/all_gather | solution.py:41
  19.7 0.1 convert_reduce_fusion.1
  19.7 0.0 copy-start
  19.8 44.3 %all-gather.4.cloned.1.call-done = bf16[768,2704]{1,0:T(8,128)(2,1)} async-done(((bf16[48,2704]{1,0:T(8,128)(2,1)}), bf16[768,2704]{1,0:T(8,128)(2,1)}) %all-gather.4.cloned.1.call-update) | async-done | bytes 4153360 | tf_op jit(solution)/shard_map/all_gather | solution.py:45
  64.1 3.6 fusion.3
  67.6 47.4 %all-gather.6.cloned.1.call-done = bf16[768,2652]{1,0:T(8,128)(2,1)} async-done(((bf16[48,2652]{1,0:T(8,128)(2,1)}), bf16[768,2652]{1,0:T(8,128)(2,1)}) %all-gather.6.cloned.1.call-update) | async-done | bytes 4073488 | tf_op jit(solution)/shard_map/all_gather | solution.py:48
  115.1 3.0 convolution_convert_fusion
  118.0 7.2 %all_to_all.5 = bf16[2,16,2652]{2,1,0:T(8,128)(2,1)S(1)} all-to-all(bf16[2,16,2652]{2,1,0:T(8,128)(2,1)S(1)} %bitcast.9), channel_id=1, replica_groups=mesh['dp'=16,'mp'=2] {'mp'}, dimensions={0} | all-to-all | bytes 339456 | tf_op jit(solution)/shard_map/all_to_all | solution.py:51
  125.3 0.0 copy-done
  125.3 1.3 fusion.1
  126.6 5.1 %all_gather.20 = bf16[32,2652]{1,0:T(8,128)(2,1)S(1)} all-gather(bf16[16,2652]{1,0:T(8,128)(2,1)S(1)} %get-tuple-element.7), channel_id=1, replica_groups=mesh['dp'=16,'mp'=2] {'mp'}, dimensions={0}, use_global_device_ids=true | all-gather | bytes 254592 | tf_op jit(solution)/shard_map/all_gather | solution.py:55
  131.8 4.5 %fusion.26 = f32[768,2652]{1,0:T(8,128)} fusion(bf16[32,2652]{1,0:T(8,128)(2,1)S(1)} %all_gather.20, f32[32,768]{1,0:T(8,128)S(1)} %fusion.3), kind=kOutput, calls=%fused_computation.40 | convolution fusion | flops 130572288 | bytes 8414976 | tf_op jit(solution)/shard_map/dot_general | solution.py:30
  136.2 0.0 reduce-scatter.5.cloned.1.call-update
  136.2 0.0 reduce-scatter.3.cloned.1.call-start
  136.3 9.1 %fusion.2 = f32[768,2704]{1,0:T(8,128)} fusion(bf16[32,52]{1,0:T(8,128)(2,1)S(1)} %convert_reduce_fusion.1, bf16[32,2652]{1,0:T(8,128)(2,1)S(1)} %all_gather.16, f32[32,768]{1,0:T(8,128)S(1)} %fusion.3, bf16[32,2652]{1,0:T(8,128)(2,1)S(1)} %all_gather.20, bf16[768,2652]{1,0:T(8,128)(2,1)} %all-gather.6.cloned.1.call-done), kind=kOutput, calls=%fused_computation.14 | convolution fusion | flops 264095744 | bytes 12821248 | tf_op jit(solution)/shard_map/dot_general | solution.py:30
  145.4 0.0 reduce-scatter.3.cloned.1.call-update
  145.5 91.6 %reduce-scatter.5.cloned.1.call-done = f32[48,2652]{1,0:T(8,128)} async-done(((f32[768,2652]{1,0:T(8,128)}), f32[48,2652]{1,0:T(8,128)}) %reduce-scatter.5.cloned.1.call-update) | async-done | bytes 509200 | tf_op jit(solution)/shard_map/reduce_scatter | solution.py:59
  237.0 1.8 multiply_reduce_fusion.1
  238.8 107.6 %reduce-scatter.3.cloned.1.call-done = f32[48,2704]{1,0:T(8,128)} async-done(((f32[768,2704]{1,0:T(8,128)}), f32[48,2704]{1,0:T(8,128)}) %reduce-scatter.3.cloned.1.call-update) | async-done | bytes 519184 | tf_op jit(solution)/shard_map/reduce_scatter | solution.py:66
  346.4 1.8 multiply_reduce_fusion
  349.5 40.5 %all-reduce = (f32[]{:T(128)}, f32[]{:T(128)}) all-reduce(f32[]{:T(128)S(6)} %add.26, f32[]{:T(128)} %get-tuple-element.6), channel_id=1, replica_groups=mesh['dp'=16,'mp'=2] {'dp','mp'}, use_global_device_ids=true, to_apply=%region_6.7 | all-reduce | flops 2 | bytes 16 | tf_op jit(solution)/shard_map/psum | solution.py:70
  391.4 1.9 broadcast_multiply_fusion.1
  393.3 1.9 broadcast_multiply_fusion
  (2 shorter events, 0.0 us)
Async XLA Ops:
  7.2 56.9 %all-gather.4.cloned.1.call-start = ((), (), s32[]{:S(2)}) async-start(), calls=%async_computation.3 | async-start | bytes 4595712 | tf_op jit(solution)/shard_map/all_gather | solution.py:45
  7.9 107.2 %all-gather.6.cloned.1.call-start = ((), (), s32[]{:S(2)}) async-start(), calls=%async_computation.4 | async-start | bytes 4386816 | tf_op jit(solution)/shard_map/all_gather | solution.py:48
  8.6 228.4 %reduce-scatter.5.cloned.1.call-start = ((), (), s32[]{:S(2)}) async-start(), calls=%async_computation.6 | async-start | bytes 8773632 | tf_op jit(solution)/shard_map/reduce_scatter | solution.py:59
  19.7 105.6 %copy-start = (bf16[16,2652]{1,0:T(8,128)(2,1)S(1)}, bf16[16,2652]{1,0:T(8,128)(2,1)}, u32[]{:S(2)}) copy-start(bf16[16,2652]{1,0:T(8,128)(2,1)} %param.7) | copy-start | bytes 254596
  136.2 210.2 %reduce-scatter.3.cloned.1.call-start = ((), (), s32[]{:S(2)}) async-start(), calls=%async_computation.5 | async-start | bytes 9191424 | tf_op jit(solution)/shard_map/reduce_scatter | solution.py:66
Sparse Core Ops, SparseCore 0:
  10.3 53.7 all-gather.3
  66.4 48.6 all-gather.5
  136.4 100.6 reduce-scatter.4
  241.0 105.4 reduce-scatter.2
where the time goes:
time: 403 us
  waiting for transfers between devices  292 us (72%)
  blocking collectives  63.8 us (16%)
  matrix products  20.1 us (5%)
  between operations  17.6 us (4%)
  other arithmetic  8.71 us (2%)
    reduce_scatter x1, waiting for transfers between devices, body(): lax.psum_scatter(left_product(preact_grad, features), 'dp', scatter_dimen...  108 us
    reduce_scatter x1, waiting for transfers between devices, body(): lax.psum_scatter(left_product(hidden, out_grad), 'dp', scatter_dimension=...  91.6 us
    all_gather x1, waiting for transfers between devices, body(): local_out = lax.all_gather(w_out, 'dp', axis=0, tiled=True)  47.4 us
    all_gather x1, waiting for transfers between devices, body(): local_in = lax.all_gather(w_in, 'dp', axis=0, tiled=True)  44.3 us
    psum x1, blocking collectives, body(): square_total = lax.psum(square_part, ('dp', 'mp'))  40.5 us
    dot_general x2, matrix products, left_product(): lax.dot_general(left_side, right_side, (((0,), (0,)), ((), ())), preferre...  13.6 us
  transfers between devices with their start and end apart: 4, of which 4 were waited for; matrix products, arithmetic and copies ran while one was open for 4% of the time, Pallas kernels for 0%

commit v1 on v0

v1 whole, which is shorter than its diff:
```python
import jax
import jax.numpy as jnp
from jax import lax
from jax.sharding import PartitionSpec as P

CARDS = 52


def huber_terms(error_value):
    magnitude = jnp.abs(error_value)
    return jnp.where(magnitude <= 1.0, 0.5 * error_value * error_value, magnitude - 0.5)


def build_features(ranges, board):
    card_ids = jnp.arange(CARDS, dtype=jnp.int32)
    onehot_board = jnp.sum(
        (board[:, :, None] == card_ids[None, None, :]).astype(jnp.float32), axis=1
    ).astype(jnp.bfloat16)
    return jnp.concatenate([ranges, onehot_board], axis=1)


def right_product(left_side, right_block):
    return lax.dot_general(
        left_side, right_block, (((1,), (1,)), ((), ())), preferred_element_type=jnp.float32
    )


def left_product(left_side, right_side):
    return lax.dot_general(
        left_side, right_side, (((0,), (0,)), ((), ())), preferred_element_type=jnp.float32
    )


def gather_weights_body(ranges, board, targets, w_in, w_out):
    mp_count = lax.axis_size("mp")
    dp_count = lax.axis_size("dp")
    stored_rows = ranges.shape[0]
    value_width = w_out.shape[1]
    all_ranges = lax.all_gather(ranges, "mp", axis=0, tiled=True)
    all_board = lax.all_gather(board, "mp", axis=0, tiled=True)
    features = build_features(all_ranges, all_board)
    local_in = lax.all_gather(w_in, "dp", axis=0, tiled=True)
    preact = right_product(features, local_in)
    hidden = jax.nn.gelu(preact).astype(jnp.bfloat16)
    local_out = lax.all_gather(w_out, "dp", axis=0, tiled=True)
    partial_value = jnp.dot(hidden, local_out, preferred_element_type=jnp.float32)
    stacked = partial_value.astype(jnp.bfloat16).reshape(mp_count, stored_rows, value_width)
    received = lax.all_to_all(stacked, "mp", split_axis=0, concat_axis=0, tiled=True)
    summed = jnp.sum(received.astype(jnp.float32), axis=0)
    error_value = summed - targets.astype(jnp.float32)
    own_grad = jnp.clip(error_value, -1.0, 1.0).astype(jnp.bfloat16)
    out_grad = lax.all_gather(own_grad, "mp", axis=0, tiled=True)
    predicted = summed.astype(jnp.bfloat16)
    loss_part = jnp.sum(huber_terms(error_value))
    grad_out = lax.psum_scatter(
        left_product(hidden, out_grad), "dp", scatter_dimension=0, tiled=True
    )
    hidden_grad = right_product(out_grad, local_out)
    unused_value, gelu_back = jax.vjp(jax.nn.gelu, preact)
    preact_grad = gelu_back(hidden_grad)[0].astype(jnp.bfloat16)
    grad_in = lax.psum_scatter(
        left_product(preact_grad, features), "dp", scatter_dimension=0, tiled=True
    )
    square_part = jnp.sum(grad_in * grad_in) + jnp.sum(grad_out * grad_out)
    loss_total, square_total = lax.psum((loss_part, square_part), ("dp", "mp"))
    device_count = mp_count * dp_count
    count_params = w_in.shape[0] * device_count * (w_in.shape[1] + value_width)
    scale = lax.rsqrt(square_total / count_params + 1e-06)
    loss = loss_total / (stored_rows * device_count * value_width)
    return (predicted, grad_in * scale, grad_out * scale, loss)


def gather_states_body(ranges, board, targets, w_in, w_out):
    axes = ("dp", "mp")
    device_count = lax.axis_size("dp") * lax.axis_size("mp")
    stored_rows = ranges.shape[0]
    value_width = w_out.shape[1]
    features = lax.all_gather(build_features(ranges, board), axes, axis=0, tiled=True)
    preact = right_product(features, w_in)
    hidden = jax.nn.gelu(preact).astype(jnp.bfloat16)
    partial_value = jnp.dot(hidden, w_out, preferred_element_type=jnp.float32)
    summed = lax.psum_scatter(
        partial_value.astype(jnp.bfloat16), axes, scatter_dimension=0, tiled=True
    ).astype(jnp.float32)
    error_value = summed - targets.astype(jnp.float32)
    own_grad = jnp.clip(error_value, -1.0, 1.0).astype(jnp.bfloat16)
    out_grad = lax.all_gather(own_grad, axes, axis=0, tiled=True)
    predicted = summed.astype(jnp.bfloat16)
    loss_part = jnp.sum(huber_terms(error_value))
    grad_out = left_product(hidden, out_grad)
    hidden_grad = right_product(out_grad, w_out)
    unused_value, gelu_back = jax.vjp(jax.nn.gelu, preact)
    preact_grad = gelu_back(hidden_grad)[0].astype(jnp.bfloat16)
    grad_in = left_product(preact_grad, features)
    square_part = jnp.sum(grad_in * grad_in) + jnp.sum(grad_out * grad_out)
    loss_total, square_total = lax.psum((loss_part, square_part), axes)
    count_params = w_in.shape[0] * device_count * (w_in.shape[1] + value_width)
    scale = lax.rsqrt(square_total / count_params + 1e-06)
    loss = loss_total / (stored_rows * device_count * value_width)
    return (predicted, grad_in * scale, grad_out * scale, loss)


def solution(mesh):
    rows = P(("dp", "mp"), None)
    units = P(("mp", "dp"), None)

    def step(ranges, board, targets, w_in, w_out):
        batch_fits = ranges.shape[0] <= w_in.shape[0] // mesh.shape["mp"]
        body = gather_states_body if batch_fits else gather_weights_body
        mapped = jax.shard_map(
            body,
            mesh=mesh,
            in_specs=(rows, rows, rows, units, units),
            out_specs=(rows, units, units, P()),
            check_vma=False,
        )
        return mapped(ranges, board, targets, w_in, w_out)

    return step
```

time: 403 us -> 298 us (0.74)
  waiting for transfers between devices: 292 us -> 222 us
  blocking collectives: 63.8 us -> 38.5 us
  matrix products: 20.1 us -> 13 us
    reduce_scatter x2 -> x1, waiting for transfers between devices: 199 us -> 100 us  [gather_states_body(): lax.psum_scatter(partial_value.astype(jnp.bfloat16), axes, scatter_dimens...]
    all_gather x2, waiting for transfers between devices: 91.7 us -> 121 us  [the longest x1 63 us: gather_states_body(): lax.all_gather(build_features(ranges, board), axes, axis=0, tiled=True)]
    all_gather x3 -> x0, blocking collectives: 16 us -> none  [the longest x1 5.52 us: body(): lax.all_gather(board, 'mp', axis=0, tiled=True)]
    all_to_all x1 -> x0, blocking collectives: 7.25 us -> none  [body(): lax.all_to_all(stacked, 'mp', split_axis=0, concat_axis=0, tiled=True)]
    dot_general x2, matrix products: 13.6 us -> 7.71 us  [left_product(): lax.dot_general(left_side, right_side, (((0,), (0,)), ((), ())), preferre...]
  transfers between devices with their start and end apart: 4 -> 3, of which waited for: 4 -> 3; matrix products, arithmetic and copies ran while one was open for 4% -> 0% of each run, Pallas kernels for 0% -> 0%
where the time goes in v1:
time: 298 us; the launch traced here: 297 us
  waiting for transfers between devices  222 us (74%)
  blocking collectives  38.5 us (13%)
  between operations  17.6 us (6%)
  matrix products  13 us (4%)
  other arithmetic  6.3 us (2%)
    reduce_scatter x1, waiting for transfers between devices, gather_states_body(): lax.psum_scatter(partial_value.astype(jnp.bfloat16), axes, scatter_dimens...  100 us
    all_gather x1, waiting for transfers between devices, gather_states_body(): lax.all_gather(build_features(ranges, board), axes, axis=0, tiled=True)  63 us
    all_gather x1, waiting for transfers between devices, gather_states_body(): out_grad = lax.all_gather(own_grad, axes, axis=0, tiled=True)  58.4 us
    psum x1, blocking collectives, gather_states_body(): loss_total, square_total = lax.psum((loss_part, square_part), axes)  38.5 us
    dot_general x2, matrix products, left_product(): lax.dot_general(left_side, right_side, (((0,), (0,)), ((), ())), preferre...  7.71 us
  transfers between devices with their start and end apart: 3, of which 3 were waited for; matrix products, arithmetic and copies ran while one was open for 0% of the time, Pallas kernels for 0%

profile of v1, /device:TPU:0, one launch (start us, length us, event | category | flops | bytes accessed | tf_op | source)
XLA Modules:
  0.0 297.5 jit_solution(3232524638307259648)
XLA Ops:
  7.2 0.0 copy-start
  7.2 0.0 copy-start.3
  7.2 0.0 all-gather.3.cloned.1.call-start
  7.2 0.8 convert_reduce_fusion
  8.1 1.6 pad_maximum_fusion
  9.7 0.0 all-gather.3.cloned.1.call-update
  9.7 0.0 reduce-scatter.2.cloned.1.call-start
  9.7 63.0 %all-gather.3.cloned.1.call-done = bf16[512,2704]{1,0:T(8,128)(2,1)} async-done(((bf16[16,2704]{1,0:T(8,128)(2,1)}), bf16[512,2704]{1,0:T(8,128)(2,1)}) %all-gather.3.cloned.1.call-update) | async-done | bytes 2768912 | tf_op jit(solution)/shard_map/all_gather | solution.py:78
  72.7 0.0 copy-done
  72.7 2.8 fusion.26
  75.5 0.0 copy-done.3
  75.5 0.0 copy-start.1
  75.5 2.5 convolution_convert_fusion
  78.0 0.0 reduce-scatter.2.cloned.1.call-update
  78.0 0.0 all-gather.5.cloned.1.call-start
  78.1 100.4 %reduce-scatter.2.cloned.1.call-done = bf16[16,2652]{1,0:T(8,128)(2,1)} async-done(((bf16[512,2652]{1,0:T(8,128)(2,1)}), bf16[16,2652]{1,0:T(8,128)(2,1)}) %reduce-scatter.2.cloned.1.call-update) | async-done | bytes 84880 | tf_op jit(solution)/shard_map/reduce_scatter | solution.py:82
  178.5 2.2 fusion.1
  180.7 0.0 all-gather.5.cloned.1.call-update
  180.8 58.4 %all-gather.5.cloned.1.call-done = bf16[512,2652]{1,0:T(8,128)(2,1)} async-done(((bf16[16,2652]{1,0:T(8,128)(2,1)}), bf16[512,2652]{1,0:T(8,128)(2,1)}) %all-gather.5.cloned.1.call-update) | async-done | bytes 2715664 | tf_op jit(solution)/shard_map/all_gather | solution.py:87
  239.2 0.0 copy-done.1
  239.2 4.6 %multiply_reduce_fusion = (f32[]{:T(128)}, f32[48,2704]{1,0:T(8,128)}) fusion(bf16[512,2704]{1,0:T(8,128)(2,1)S(1)} %copy-done.1, f32[512,48]{0,1:T(8,128)S(1)} %fusion.26, bf16[512,2652]{1,0:T(8,128)(2,1)} %all-gather.5.cloned.1.call-done, bf16[48,2652]{1,0:T(8,128)(2,1)S(1)} %copy-done.3), kind=kOutput, calls=%fused_computation.1 | convolution fusion | flops 264009216 | bytes 6356612 | tf_op jit(solution)/shard_map/dot_general | solution.py:29
  243.8 0.0 copy-start.2
  243.8 3.1 %multiply_reduce_fusion.1 = (f32[]{:T(128)}, f32[48,2652]{1,0:T(8,128)S(1)}) fusion(bf16[512,2652]{1,0:T(8,128)(2,1)} %all-gather.5.cloned.1.call-done, f32[512,48]{0,1:T(8,128)S(1)} %fusion.26), kind=kOutput, calls=%fused_computation.2 | convolution fusion | flops 130826880 | bytes 3323140 | tf_op jit(solution)/shard_map/dot_general | solution.py:29
  248.3 38.5 %all-reduce = (f32[]{:T(128)}, f32[]{:T(128)}) all-reduce(f32[]{:T(128)S(6)} %add.24, f32[]{:T(128)} %get-tuple-element.6), channel_id=1, replica_groups=mesh['dp'=16,'mp'=2] {'dp','mp'}, use_global_device_ids=true, to_apply=%region_4.5 | all-reduce | flops 2 | bytes 16 | tf_op jit(solution)/shard_map/psum | solution.py:96
  287.5 0.8 broadcast_multiply_fusion.1
  288.3 0.0 copy-done.2
  288.3 0.8 broadcast_multiply_fusion
Async XLA Ops:
  7.2 65.5 %copy-start = (bf16[48,2704]{1,0:T(8,128)(2,1)S(1)}, bf16[48,2704]{1,0:T(8,128)(2,1)}, u32[]{:S(2)}) copy-start(bf16[48,2704]{1,0:T(8,128)(2,1)} %param.8) | copy-start | bytes 778756
  7.2 68.3 %copy-start.3 = (bf16[48,2652]{1,0:T(8,128)(2,1)S(1)}, bf16[48,2652]{1,0:T(8,128)(2,1)}, u32[]{:S(2)}) copy-start(bf16[48,2652]{1,0:T(8,128)(2,1)} %param.9) | copy-start | bytes 763780
  7.2 65.5 %all-gather.3.cloned.1.call-start = ((), (), s32[]{:S(2)}) async-start(), calls=%async_computation.1 | async-start | bytes 2973696 | tf_op jit(solution)/shard_map/all_gather | solution.py:78
  9.7 168.8 %reduce-scatter.2.cloned.1.call-start = ((), (), s32[]{:S(2)}) async-start(), calls=%async_computation.2 | async-start | bytes 2838528 | tf_op jit(solution)/shard_map/reduce_scatter | solution.py:82
  75.5 163.7 %copy-start.1 = (bf16[512,2704]{1,0:T(8,128)(2,1)S(1)}, bf16[512,2704]{1,0:T(8,128)(2,1)}, u32[]{:S(2)}) copy-start(bf16[512,2704]{1,0:T(8,128)(2,1)} %all-gather.3.cloned.1.call-done) | copy-start | bytes 8306692
  78.0 161.2 %all-gather.5.cloned.1.call-start = ((), (), s32[]{:S(2)}) async-start(), calls=%async_computation.3 | async-start | bytes 2838528 | tf_op jit(solution)/shard_map/all_gather | solution.py:87
  243.8 44.5 %copy-start.2 = (f32[48,2704]{1,0:T(8,128)S(1)}, f32[48,2704]{1,0:T(8,128)}, u32[]{:S(2)}) copy-start(f32[48,2704]{1,0:T(8,128)} %get-tuple-element.9) | copy-start | bytes 1557508
Sparse Core Ops, SparseCore 0:
  11.4 61.2 all-gather.2
  78.6 99.8 reduce-scatter.1
  182.0 57.1 all-gather.4

commit v2 on v1

--- a/solution.py
+++ b/solution.py
@@ -70,46 +70,96 @@
     return (predicted, grad_in * scale, grad_out * scale, loss)
 
 
-def gather_states_body(ranges, board, targets, w_in, w_out):
-    axes = ("dp", "mp")
-    device_count = lax.axis_size("dp") * lax.axis_size("mp")
+def exchange(block, axes, step):
+    count = lax.axis_size(axes)
+    return lax.ppermute(block, axes, [(index, index ^ step) for index in range(count)])
+
+
+def gather_blocks(block, axes):
+    return [block] + [exchange(block, axes, step) for step in range(1, lax.axis_size(axes))]
+
+
+def scatter_sum(blocks, axes):
+    total = blocks[0]
+    received = [
+        exchange(blocks[step].astype(jnp.bfloat16), axes, step)
+        for step in range(1, lax.axis_size(axes))
+    ]
+    for part in received:
+        total = total + part.astype(jnp.float32)
+    return total
+
+
+def split_rows(whole, count):
+    size = whole.shape[0] // count
+    return [whole[index * size : (index + 1) * size] for index in range(count)]
+
+
+def gather_states(rows):
+    near = gather_blocks(rows, ("z",))
+    far = [exchange(block, ("c",), 1) for block in near]
+    return jnp.concatenate(near + far, axis=0)
+
+
+def torus_body(ranges, board, targets, w_in, w_out):
+    plane = ("x", "y")
+    z_count = lax.axis_size("z")
+    plane_count = lax.axis_size(plane)
+    device_count = z_count * plane_count * lax.axis_size("c")
     stored_rows = ranges.shape[0]
     value_width = w_out.shape[1]
-    features = lax.all_gather(build_features(ranges, board), axes, axis=0, tiled=True)
-    preact = right_product(features, w_in)
+    units_in = jnp.concatenate(gather_blocks(w_in, plane), axis=0)
+    features = gather_states(build_features(ranges, board))
+    units_out = jnp.concatenate(gather_blocks(w_out, plane), axis=0)
+    preact = right_product(features, units_in)
     hidden = jax.nn.gelu(preact).astype(jnp.bfloat16)
-    partial_value = jnp.dot(hidden, w_out, preferred_element_type=jnp.float32)
-    summed = lax.psum_scatter(
-        partial_value.astype(jnp.bfloat16), axes, scatter_dimension=0, tiled=True
-    ).astype(jnp.float32)
+    partial_value = jnp.dot(hidden, units_out, preferred_element_type=jnp.float32)
+    own_half, other_half = split_rows(partial_value, 2)
+    chip_value = own_half + exchange(other_half.astype(jnp.bfloat16), ("c",), 1).astype(jnp.float32)
+    summed = scatter_sum(split_rows(chip_value, z_count), ("z",))
     error_value = summed - targets.astype(jnp.float32)
-    own_grad = jnp.clip(error_value, -1.0, 1.0).astype(jnp.bfloat16)
-    out_grad = lax.all_gather(own_grad, axes, axis=0, tiled=True)
+    out_grad = gather_states(jnp.clip(error_value, -1.0, 1.0).astype(jnp.bfloat16))
     predicted = summed.astype(jnp.bfloat16)
     loss_part = jnp.sum(huber_terms(error_value))
-    grad_out = left_product(hidden, out_grad)
-    hidden_grad = right_product(out_grad, w_out)
+    grad_out = scatter_sum(split_rows(left_product(hidden, out_grad), plane_count), plane)
+    hidden_grad = right_product(out_grad, units_out)
     unused_value, gelu_back = jax.vjp(jax.nn.gelu, preact)
     preact_grad = gelu_back(hidden_grad)[0].astype(jnp.bfloat16)
-    grad_in = left_product(preact_grad, features)
+    grad_in = scatter_sum(split_rows(left_product(preact_grad, features), plane_count), plane)
     square_part = jnp.sum(grad_in * grad_in) + jnp.sum(grad_out * grad_out)
-    loss_total, square_total = lax.psum((loss_part, square_part), axes)
+    lane = lax.broadcasted_iota(jnp.int32, (device_count, 128), 1)
+    copies = jnp.where(lane == 0, square_part, jnp.where(lane == 1, loss_part, 0.0))
+    totals = jnp.sum(
+        lax.all_to_all(copies, ("z", "x", "c", "y"), split_axis=0, concat_axis=0, tiled=True), axis=0
+    )
     count_params = w_in.shape[0] * device_count * (w_in.shape[1] + value_width)
-    scale = lax.rsqrt(square_total / count_params + 1e-06)
-    loss = loss_total / (stored_rows * device_count * value_width)
+    scale = lax.rsqrt(totals[0] / count_params + 1e-06)
+    loss = totals[1] / (stored_rows * device_count * value_width)
     return (predicted, grad_in * scale, grad_out * scale, loss)
 
 
+def torus_mesh(mesh):
+    devices = mesh.devices
+    chips = [tuple(device.coords) for device in devices.flat]
+    z_count = len({chip[2] for chip in chips})
+    x_count = len({chip[0] for chip in chips})
+    core_count = devices.size // len(set(chips))
+    shape = (z_count, x_count, core_count, devices.shape[1])
+    return jax.sharding.Mesh(devices.reshape(shape), ("z", "x", "c", "y"))
+
+
 def solution(mesh):
-    rows = P(("dp", "mp"), None)
-    units = P(("mp", "dp"), None)
-
     def step(ranges, board, targets, w_in, w_out):
         batch_fits = ranges.shape[0] <= w_in.shape[0] // mesh.shape["mp"]
-        body = gather_states_body if batch_fits else gather_weights_body
+        if batch_fits:
+            used_mesh, body = torus_mesh(mesh), torus_body
+            rows, units = P(("z", "x", "c", "y"), None), P(("y", "z", "x", "c"), None)
+        else:
+            used_mesh, body = mesh, gather_weights_body
+            rows, units = P(("dp", "mp"), None), P(("mp", "dp"), None)
         mapped = jax.shard_map(
             body,
-            mesh=mesh,
+            mesh=used_mesh,
             in_specs=(rows, rows, rows, units, units),
             out_specs=(rows, units, units, P()),
             check_vma=False,

time: 298 us -> 120 us (0.40)
  waiting for transfers between devices: 222 us -> 57.9 us
  starting transfers between devices: 0.12 us -> 29.4 us
  blocking collectives: 38.5 us -> 10 us
  between operations: 17.6 us -> 4.73 us
  matrix products: 13 us -> 5.28 us
    all_gather x2 -> x0, waiting for transfers between devices: 121 us -> none  [the longest x1 63 us: gather_states_body(): lax.all_gather(build_features(ranges, board), axes, axis=0, tiled=True)]
    reduce_scatter x1 -> x0, waiting for transfers between devices: 100 us -> none  [gather_states_body(): lax.psum_scatter(partial_value.astype(jnp.bfloat16), axes, scatter_dimens...]
    ppermute x0 -> x30, waiting for transfers between devices: none -> 57.9 us  [exchange(): lax.ppermute(block, axes, [(index, index ^ step) for index in range(count)])]
    psum x1 -> x0, blocking collectives: 38.5 us -> none  [gather_states_body(): loss_total, square_total = lax.psum((loss_part, square_part), axes)]
    ppermute x0 -> x30, starting transfers between devices: none -> 29.4 us  [exchange(): lax.ppermute(block, axes, [(index, index ^ step) for index in range(count)])]
    all_to_all x0 -> x1, blocking collectives: none -> 10 us  [torus_body(): lax.all_to_all(copies, ('z', 'x', 'c', 'y'), split_axis=0, concat_axis=0,...]
    dot_general x2, matrix products: 7.71 us -> 4.18 us  [left_product(): lax.dot_general(left_side, right_side, (((0,), (0,)), ((), ())), preferre...]
  transfers between devices with their start and end apart: 3 -> 30, of which waited for: 3 -> 17; matrix products, arithmetic and copies ran while one was open for 0% -> 5% of each run, Pallas kernels for 0% -> 0%
where the time goes in v2:
time: 120 us; the launch traced here: 119 us
  waiting for transfers between devices  57.9 us (48%)
  starting transfers between devices  29.4 us (24%)
  blocking collectives  10 us (8%)
  other arithmetic  9.23 us (8%)
  matrix products  5.28 us (4%)
  between operations  4.73 us (4%)
  local copies, waits for them, and re-layouts  2.9 us (2%)
    ppermute x30, waiting for transfers between devices, exchange(): lax.ppermute(block, axes, [(index, index ^ step) for index in range(count)])  57.9 us
    ppermute x30, starting transfers between devices, exchange(): lax.ppermute(block, axes, [(index, index ^ step) for index in range(count)])  29.4 us
    all_to_all x1, blocking collectives, torus_body(): lax.all_to_all(copies, ('z', 'x', 'c', 'y'), split_axis=0, concat_axis=0,...  10 us
    dot_general x2, matrix products, left_product(): lax.dot_general(left_side, right_side, (((0,), (0,)), ((), ())), preferre...  4.18 us
    mul x2, other arithmetic, torus_body(): return (predicted, grad_in * scale, grad_out * scale, loss)  2.9 us
  transfers between devices with their start and end apart: 30, of which 17 were waited for; matrix products, arithmetic and copies ran while one was open for 5% of the time, Pallas kernels for 0%

profile of v2, /device:TPU:0, one launch (start us, length us, event | category | flops | bytes accessed | tf_op | source)
XLA Modules:
  0.0 119.5 jit_solution(695868395307394930)
XLA Ops:
  0.6 3.0 %collective-permute-start.11 = (bf16[48,2652]{1,0:T(8,128)(2,1)}, bf16[48,2652]{1,0:T(8,128)(2,1)S(1)}, u32[]{:S(2)}, u32[]{:S(2)}) collective-permute-start(bf16[48,2652]{1,0:T(8,128)(2,1)} %param.9), channel_id=1, source_target_pairs={{0,4},{1,5},{4,0},{5,1},{2,6},{3,7},{6,2},{7,3},{8,12},{9,13},{12,... | collective-permute-start | bytes 763784 | tf_op jit(solution)/shard_map/ppermute | solution.py:75
  3.7 1.5 %collective-permute-start.10 = (bf16[48,2652]{1,0:T(8,128)(2,1)}, bf16[48,2652]{1,0:T(8,128)(2,1)S(1)}, u32[]{:S(2)}, u32[]{:S(2)}) collective-permute-start(bf16[48,2652]{1,0:T(8,128)(2,1)} %param.9), channel_id=1, source_target_pairs={{0,1},{1,0},{4,5},{5,4},{2,3},{3,2},{6,7},{7,6},{8,9},{9,8},{12,13... | collective-permute-start | bytes 763784 | tf_op jit(solution)/shard_map/ppermute | solution.py:75
  5.2 0.0 collective-permute-start.12
  5.2 0.8 convert_reduce_fusion
  6.0 1.0 pad_maximum_fusion
  7.0 4.1 %collective-permute-start.2 = (bf16[16,2704]{1,0:T(8,128)(2,1)S(1)}, bf16[16,2704]{1,0:T(8,128)(2,1)S(1)}, u32[]{:S(2)}, u32[]{:S(2)}) collective-permute-start(bf16[16,2704]{1,0:T(8,128)(2,1)S(1)} %get-tuple-element.36), channel_id=1, source_target_pairs={{0,24},{8,16},{16,8},{24,0},{1,25},{9,17},{17,9},{25,1},{2,26},{10... | collective-permute-start | bytes 259592 | tf_op jit(solution)/shard_map/ppermute | solution.py:75
  11.0 1.0 constant_dynamic-update-slice_fusion.11
  12.0 3.6 %collective-permute-done = bf16[16,2704]{1,0:T(8,128)(2,1)S(1)} collective-permute-done((bf16[16,2704]{1,0:T(8,128)(2,1)S(1)}, bf16[16,2704]{1,0:T(8,128)(2,1)S(1)}, u32[]{:S(2)}, u32[]{:S(2)}) %collective-permute-start) | collective-permute-done | bytes 86560 | tf_op jit(solution)/shard_map/ppermute | solution.py:75
  15.6 6.4 %collective-permute-done.1 = bf16[16,2704]{1,0:T(8,128)(2,1)S(1)} collective-permute-done((bf16[16,2704]{1,0:T(8,128)(2,1)S(1)}, bf16[16,2704]{1,0:T(8,128)(2,1)S(1)}, u32[]{:S(2)}, u32[]{:S(2)}) %collective-permute-start.1) | collective-permute-done | bytes 86560 | tf_op jit(solution)/shard_map/ppermute | solution.py:75
  22.0 1.6 %collective-permute-start.8 = (bf16[48,2704]{1,0:T(8,128)(2,1)}, bf16[48,2704]{1,0:T(8,128)(2,1)S(1)}, u32[]{:S(2)}, u32[]{:S(2)}) collective-permute-start(bf16[48,2704]{1,0:T(8,128)(2,1)} %param.8), channel_id=1, source_target_pairs={{0,4},{1,5},{4,0},{5,1},{2,6},{3,7},{6,2},{7,3},{8,12},{9,13},{12,... | collective-permute-start | bytes 778760 | tf_op jit(solution)/shard_map/ppermute | solution.py:75
  23.5 0.3 collective-permute-start.4
  23.8 1.1 collective-permute-done.4
  24.9 0.2 collective-permute-start.5
  25.1 1.1 collective-permute-done.5
  26.2 0.2 collective-permute-start.6
  26.4 1.1 collective-permute-done.6
  27.5 1.5 %collective-permute-start.7 = (bf16[48,2704]{1,0:T(8,128)(2,1)}, bf16[48,2704]{1,0:T(8,128)(2,1)S(1)}, u32[]{:S(2)}, u32[]{:S(2)}) collective-permute-start(bf16[48,2704]{1,0:T(8,128)(2,1)} %param.8), channel_id=1, source_target_pairs={{0,1},{1,0},{4,5},{5,4},{2,3},{3,2},{6,7},{7,6},{8,9},{9,8},{12,13... | collective-permute-start | bytes 778760 | tf_op jit(solution)/shard_map/ppermute | solution.py:75
  29.0 1.1 collective-permute-start.9
  30.3 0.9 collective-permute-done.8
  31.1 11.0 %collective-permute-done.7 = bf16[48,2704]{1,0:T(8,128)(2,1)S(1)} collective-permute-done((bf16[48,2704]{1,0:T(8,128)(2,1)}, bf16[48,2704]{1,0:T(8,128)(2,1)S(1)}, u32[]{:S(2)}, u32[]{:S(2)}) %collective-permute-start.7) | collective-permute-done | bytes 259616 | tf_op jit(solution)/shard_map/ppermute | solution.py:75
  42.1 0.4 fusion
  42.6 0.7 fusion.39
  43.2 0.2 slice.112
  43.5 0.3 copy.78
  43.8 0.1 collective-permute-start.13
  43.9 0.4 copy.80
  44.3 1.3 %collective-permute-done.13 = bf16[64,2652]{1,0:T(8,128)(2,1)} collective-permute-done((bf16[64,2652]{1,0:T(8,128)(2,1)S(1)}, bf16[64,2652]{1,0:T(8,128)(2,1)}, u32[]{:S(2)}, u32[]{:S(2)}) %collective-permute-start.13) | collective-permute-done | bytes 339488 | tf_op jit(solution)/shard_map/ppermute | solution.py:75
  45.6 1.0 fusion.41
  46.7 0.2 collective-permute-start.14
  46.9 0.9 collective-permute-start.16
  47.8 2.4 %collective-permute-start.15 = (bf16[16,2652]{1,0:T(8,128)(2,1)S(1)}, bf16[16,2652]{1,0:T(8,128)(2,1)S(1)}, u32[]{:S(2)}, u32[]{:S(2)}) collective-permute-start(bf16[16,2652]{1,0:T(8,128)(2,1)S(1)} %get-tuple-element.33), channel_id=1, source_target_pairs={{0,16},{8,24},{16,0},{24,8},{1,17},{9,25},{17,1},{25,9},{2,18},{10... | collective-permute-start | bytes 254600 | tf_op jit(solution)/shard_map/ppermute | solution.py:75
  50.3 1.1 collective-permute-done.14
  51.3 2.8 %collective-permute-done.16 = bf16[16,2652]{1,0:T(8,128)(2,1)S(1)} collective-permute-done((bf16[16,2652]{1,0:T(8,128)(2,1)S(1)}, bf16[16,2652]{1,0:T(8,128)(2,1)S(1)}, u32[]{:S(2)}, u32[]{:S(2)}) %collective-permute-start.16) | collective-permute-done | bytes 84896 | tf_op jit(solution)/shard_map/ppermute | solution.py:75
  54.2 3.9 %collective-permute-done.15 = bf16[16,2652]{1,0:T(8,128)(2,1)S(1)} collective-permute-done((bf16[16,2652]{1,0:T(8,128)(2,1)S(1)}, bf16[16,2652]{1,0:T(8,128)(2,1)S(1)}, u32[]{:S(2)}, u32[]{:S(2)}) %collective-permute-start.15) | collective-permute-done | bytes 84896 | tf_op jit(solution)/shard_map/ppermute | solution.py:75
  58.1 0.1 constant_dynamic-update-slice_fusion.19
  58.1 0.1 collective-permute-start.20
  58.2 1.2 %collective-permute-start.19 = (bf16[16,2652]{1,0:T(8,128)(2,1)S(1)}, bf16[16,2652]{1,0:T(8,128)(2,1)S(1)}, u32[]{:S(2)}, u32[]{:S(2)}) collective-permute-start(bf16[16,2652]{1,0:T(8,128)(2,1)S(1)} %get-tuple-element.21), channel_id=1, source_target_pairs={{0,24},{8,16},{16,8},{24,0},{1,25},{9,17},{17,9},{25,1},{2,26},{10... | collective-permute-start | bytes 254600 | tf_op jit(solution)/shard_map/ppermute | solution.py:75
  59.5 3.2 %collective-permute-start.17 = (bf16[16,2652]{1,0:T(8,128)(2,1)S(1)}, bf16[16,2652]{1,0:T(8,128)(2,1)S(1)}, u32[]{:S(2)}, u32[]{:S(2)}) collective-permute-start(bf16[16,2652]{1,0:T(8,128)(2,1)S(1)} %get-tuple-element.21), channel_id=1, source_target_pairs={{0,8},{8,0},{16,24},{24,16},{1,9},{9,1},{17,25},{25,17},{2,10},{10... | collective-permute-start | bytes 254600 | tf_op jit(solution)/shard_map/ppermute | solution.py:75
  62.7 1.3 %fusion.13 = (f32[]{:T(128)}, bf16[16,2652]{1,0:T(8,128)(2,1)}) fusion(f32[16,2652]{1,0:T(8,128)S(1)} %get-tuple-element.22, bf16[16,2652]{1,0:T(8,128)(2,1)S(1)} %copy-done.9), kind=kLoop, calls=%fused_computation.22 | loop fusion | flops 424319 | bytes 339460 | tf_op jit(solution)/shard_map/reduce_sum | solution.py:123
  64.0 1.6 %collective-permute-done.19 = bf16[16,2652]{1,0:T(8,128)(2,1)S(1)} collective-permute-done((bf16[16,2652]{1,0:T(8,128)(2,1)S(1)}, bf16[16,2652]{1,0:T(8,128)(2,1)S(1)}, u32[]{:S(2)}, u32[]{:S(2)}) %collective-permute-start.19) | collective-permute-done | bytes 84896 | tf_op jit(solution)/shard_map/ppermute | solution.py:75
  65.6 3.0 %collective-permute-done.18 = bf16[16,2652]{1,0:T(8,128)(2,1)S(1)} collective-permute-done((bf16[16,2652]{1,0:T(8,128)(2,1)S(1)}, bf16[16,2652]{1,0:T(8,128)(2,1)S(1)}, u32[]{:S(2)}, u32[]{:S(2)}) %collective-permute-start.18) | collective-permute-done | bytes 84896 | tf_op jit(solution)/shard_map/ppermute | solution.py:75
  68.6 0.0 collective-permute-start.22
  68.7 0.5 collective-permute-start.21
  69.2 0.9 collective-permute-done.21
  70.1 3.8 %fusion.46 = (bf16[192,2704]{1,0:T(8,128)(2,1)S(1)}, f32[192,2704]{1,0:T(8,128)}) fusion(bf16[128,2704]{1,0:T(8,128)(2,1)} %copy-done.6, f32[128,192]{0,1:T(8,128)S(1)} %copy-done.8, bf16[128,2652]{1,0:T(8,128)(2,1)S(1)} %constant_dynamic-update-slice_fusion.12, bf16[192,2652]{1,0:T(8,128)(2,1)S(1)} %constant_dynamic-update-slice_fusion.8), kind=kOutput, calls=%fused_computation.85 | convolution fusion | flops 264268800 | bytes 5602816 | tf_op jit(solution)/shard_map/dot_general | solution.py:29
  73.9 0.4 fusion.47
  74.3 0.1 fusion.43
  74.4 1.6 %collective-permute-start.27 = (bf16[48,2652]{1,0:T(8,128)(2,1)S(1)}, bf16[48,2652]{1,0:T(8,128)(2,1)S(1)}, u32[]{:S(2)}, u32[]{:S(2)}) collective-permute-start(bf16[48,2652]{1,0:T(8,128)(2,1)S(1)} %get-tuple-element.28), channel_id=1, source_target_pairs={{0,1},{1,0},{4,5},{5,4},{2,3},{3,2},{6,7},{7,6},{8,9},{9,8},{12,13... | collective-permute-start | bytes 763784 | tf_op jit(solution)/shard_map/ppermute | solution.py:75
  76.0 1.0 collective-permute-start.29
  77.0 1.0 collective-permute-start.28
  78.0 0.1 fusion.42
  78.0 1.6 %collective-permute-start.24 = (bf16[48,2704]{1,0:T(8,128)(2,1)S(1)}, bf16[48,2704]{1,0:T(8,128)(2,1)S(1)}, u32[]{:S(2)}, u32[]{:S(2)}) collective-permute-start(bf16[48,2704]{1,0:T(8,128)(2,1)S(1)} %get-tuple-element.25), channel_id=1, source_target_pairs={{0,1},{1,0},{4,5},{5,4},{2,3},{3,2},{6,7},{7,6},{8,9},{9,8},{12,13... | collective-permute-start | bytes 778760 | tf_op jit(solution)/shard_map/ppermute | solution.py:75
  79.6 1.0 collective-permute-start.26
  80.6 8.5 %collective-permute-done.27 = bf16[48,2652]{1,0:T(8,128)(2,1)S(1)} collective-permute-done((bf16[48,2652]{1,0:T(8,128)(2,1)S(1)}, bf16[48,2652]{1,0:T(8,128)(2,1)S(1)}, u32[]{:S(2)}, u32[]{:S(2)}) %collective-permute-start.27) | collective-permute-done | bytes 254624 | tf_op jit(solution)/shard_map/ppermute | solution.py:75
  89.1 1.0 collective-permute-start.25
  90.1 0.6 compare_select_fusion
  90.8 0.8 multiply_reduce_fusion.1
  91.6 8.5 %collective-permute-done.24 = bf16[48,2704]{1,0:T(8,128)(2,1)S(1)} collective-permute-done((bf16[48,2704]{1,0:T(8,128)(2,1)S(1)}, bf16[48,2704]{1,0:T(8,128)(2,1)S(1)}, u32[]{:S(2)}, u32[]{:S(2)}) %collective-permute-start.24) | collective-permute-done | bytes 259616 | tf_op jit(solution)/shard_map/ppermute | solution.py:75
  100.1 1.3 %collective-permute-done.25 = bf16[48,2704]{1,0:T(8,128)(2,1)S(1)} collective-permute-done((bf16[48,2704]{1,0:T(8,128)(2,1)S(1)}, bf16[48,2704]{1,0:T(8,128)(2,1)S(1)}, u32[]{:S(2)}, u32[]{:S(2)}) %collective-permute-start.25) | collective-permute-done | bytes 259616 | tf_op jit(solution)/shard_map/ppermute | solution.py:75
  101.4 0.8 multiply_reduce_fusion
  103.5 10.0 %all_to_all.6 = f32[32,1,128]{2,1,0:T(1,128)S(1)} all-to-all(f32[32,1,128]{2,1,0:T(1,128)S(1)} %broadcast_select_fusion), channel_id=1, replica_groups=mesh['z'=4,'x'=2,'c'=2,'y'=2] {'z','x','c','y'}, dimensions={0} | all-to-all | bytes 32768 | tf_op jit(solution)/shard_map/all_to_all | solution.py:133
  113.5 0.6 fusion.45
  115.4 0.9 broadcast_multiply_fusion
  116.4 2.0 %broadcast_multiply_fusion.1 = f32[48,2652]{1,0:T(8,128)} fusion(f32[]{:T(128)} %bitcast.1, bf16[48,2652]{1,0:T(8,128)(2,1)S(1)} %copy-done.3, bf16[48,2652]{1,0:T(8,128)(2,1)S(1)} %copy-done.5, bf16[48,2652]{1,0:T(8,128)(2,1)S(1)} %collective-permute-done.27, f32[192,2652]{1,0:T(8,128)} %copy-done.1), kind=kLoop, calls=%fused_computation.19 | loop fusion | flops 891072 | bytes 1782148 | tf_op jit(solution)/shard_map/mul | solution.py:138
  (61 shorter events, 0.4 us)
Async XLA Ops:
  0.6 41.5 %copy-start.10 = (bf16[48,2704]{1,0:T(8,128)(2,1)S(1)}, bf16[48,2704]{1,0:T(8,128)(2,1)}, u32[]{:S(2)}) copy-start(bf16[48,2704]{1,0:T(8,128)(2,1)} %param.8) | copy-start | bytes 778756
  0.6 29.5 %collective-permute-start.11 = (bf16[48,2652]{1,0:T(8,128)(2,1)}, bf16[48,2652]{1,0:T(8,128)(2,1)S(1)}, u32[]{:S(2)}, u32[]{:S(2)}) collective-permute-start(bf16[48,2652]{1,0:T(8,128)(2,1)} %param.9), channel_id=1, source_target_pairs={{0,4},{1,5},{4,0},{5,1},{2,6},{3,7},{6,2},{7,3},{8,12},{9,13},{12,... | collective-permute-start | bytes 763784 | tf_op jit(solution)/shard_map/ppermute | solution.py:75
  3.7 25.3 %collective-permute-start.10 = (bf16[48,2652]{1,0:T(8,128)(2,1)}, bf16[48,2652]{1,0:T(8,128)(2,1)S(1)}, u32[]{:S(2)}, u32[]{:S(2)}) collective-permute-start(bf16[48,2652]{1,0:T(8,128)(2,1)} %param.9), channel_id=1, source_target_pairs={{0,1},{1,0},{4,5},{5,4},{2,3},{3,2},{6,7},{7,6},{8,9},{9,8},{12,13... | collective-permute-start | bytes 763784 | tf_op jit(solution)/shard_map/ppermute | solution.py:75
  5.2 25.0 %collective-permute-start.12 = (bf16[48,2652]{1,0:T(8,128)(2,1)}, bf16[48,2652]{1,0:T(8,128)(2,1)S(1)}, u32[]{:S(2)}, u32[]{:S(2)}) collective-permute-start(bf16[48,2652]{1,0:T(8,128)(2,1)} %param.9), channel_id=1, source_target_pairs={{0,5},{1,4},{4,1},{5,0},{2,7},{3,6},{6,3},{7,2},{8,13},{9,12},{12,... | collective-permute-start | bytes 763784 | tf_op jit(solution)/shard_map/ppermute | solution.py:75
  7.0 15.0 %collective-permute-start.2 = (bf16[16,2704]{1,0:T(8,128)(2,1)S(1)}, bf16[16,2704]{1,0:T(8,128)(2,1)S(1)}, u32[]{:S(2)}, u32[]{:S(2)}) collective-permute-start(bf16[16,2704]{1,0:T(8,128)(2,1)S(1)} %get-tuple-element.36), channel_id=1, source_target_pairs={{0,24},{8,16},{16,8},{24,0},{1,25},{9,17},{17,9},{25,1},{2,26},{10... | collective-permute-start | bytes 259592 | tf_op jit(solution)/shard_map/ppermute | solution.py:75
  11.0 4.5 %collective-permute-start = (bf16[16,2704]{1,0:T(8,128)(2,1)S(1)}, bf16[16,2704]{1,0:T(8,128)(2,1)S(1)}, u32[]{:S(2)}, u32[]{:S(2)}) collective-permute-start(bf16[16,2704]{1,0:T(8,128)(2,1)S(1)} %get-tuple-element.36), channel_id=1, source_target_pairs={{0,8},{8,0},{16,24},{24,16},{1,9},{9,1},{17,25},{25,17},{2,10},{10... | collective-permute-start | bytes 259592 | tf_op jit(solution)/shard_map/ppermute | solution.py:75
  15.5 6.4 %collective-permute-start.1 = (bf16[16,2704]{1,0:T(8,128)(2,1)S(1)}, bf16[16,2704]{1,0:T(8,128)(2,1)S(1)}, u32[]{:S(2)}, u32[]{:S(2)}) collective-permute-start(bf16[16,2704]{1,0:T(8,128)(2,1)S(1)} %get-tuple-element.36), channel_id=1, source_target_pairs={{0,16},{8,24},{16,0},{24,8},{1,17},{9,25},{17,1},{25,9},{2,18},{10... | collective-permute-start | bytes 259592 | tf_op jit(solution)/shard_map/ppermute | solution.py:75
  21.9 1.6 %collective-permute-start.3 = (bf16[16,2704]{1,0:T(8,128)(2,1)S(1)}, bf16[16,2704]{1,0:T(8,128)(2,1)S(1)}, u32[]{:S(2)}, u32[]{:S(2)}) collective-permute-start(bf16[16,2704]{1,0:T(8,128)(2,1)S(1)} %get-tuple-element.36), channel_id=1, source_target_pairs={{0,2},{2,0},{1,3},{3,1},{4,6},{6,4},{5,7},{7,5},{8,10},{10,8},{9,1... | collective-permute-start | bytes 259592 | tf_op jit(solution)/shard_map/ppermute | solution.py:75
  22.0 9.2 %collective-permute-start.8 = (bf16[48,2704]{1,0:T(8,128)(2,1)}, bf16[48,2704]{1,0:T(8,128)(2,1)S(1)}, u32[]{:S(2)}, u32[]{:S(2)}) collective-permute-start(bf16[48,2704]{1,0:T(8,128)(2,1)} %param.8), channel_id=1, source_target_pairs={{0,4},{1,5},{4,0},{5,1},{2,6},{3,7},{6,2},{7,3},{8,12},{9,13},{12,... | collective-permute-start | bytes 778760 | tf_op jit(solution)/shard_map/ppermute | solution.py:75
  23.5 1.4 %collective-permute-start.4 = (bf16[16,2704]{1,0:T(8,128)(2,1)S(1)}, bf16[16,2704]{1,0:T(8,128)(2,1)S(1)}, u32[]{:S(2)}, u32[]{:S(2)}) collective-permute-start(bf16[16,2704]{1,0:T(8,128)(2,1)S(1)} %collective-permute-done), channel_id=1, source_target_pairs={{0,2},{2,0},{1,3},{3,1},{4,6},{6,4},{5,7},{7,5},{8,10},{10,8},{9,1... | collective-permute-start | bytes 259592 | tf_op jit(solution)/shard_map/ppermute | solution.py:75
  24.9 1.3 %collective-permute-start.5 = (bf16[16,2704]{1,0:T(8,128)(2,1)S(1)}, bf16[16,2704]{1,0:T(8,128)(2,1)S(1)}, u32[]{:S(2)}, u32[]{:S(2)}) collective-permute-start(bf16[16,2704]{1,0:T(8,128)(2,1)S(1)} %collective-permute-done.1), channel_id=1, source_target_pairs={{0,2},{2,0},{1,3},{3,1},{4,6},{6,4},{5,7},{7,5},{8,10},{10,8},{9,1... | collective-permute-start | bytes 259592 | tf_op jit(solution)/shard_map/ppermute | solution.py:75
  26.2 1.3 %collective-permute-start.6 = (bf16[16,2704]{1,0:T(8,128)(2,1)S(1)}, bf16[16,2704]{1,0:T(8,128)(2,1)S(1)}, u32[]{:S(2)}, u32[]{:S(2)}) collective-permute-start(bf16[16,2704]{1,0:T(8,128)(2,1)S(1)} %collective-permute-done.2), channel_id=1, source_target_pairs={{0,2},{2,0},{1,3},{3,1},{4,6},{6,4},{5,7},{7,5},{8,10},{10,8},{9,1... | collective-permute-start | bytes 259592 | tf_op jit(solution)/shard_map/ppermute | solution.py:75
  27.5 14.6 %collective-permute-start.7 = (bf16[48,2704]{1,0:T(8,128)(2,1)}, bf16[48,2704]{1,0:T(8,128)(2,1)S(1)}, u32[]{:S(2)}, u32[]{:S(2)}) collective-permute-start(bf16[48,2704]{1,0:T(8,128)(2,1)} %param.8), channel_id=1, source_target_pairs={{0,1},{1,0},{4,5},{5,4},{2,3},{3,2},{6,7},{7,6},{8,9},{9,8},{12,13... | collective-permute-start | bytes 778760 | tf_op jit(solution)/shard_map/ppermute | solution.py:75
  29.0 13.5 %copy-start.6 = (bf16[128,2704]{1,0:T(8,128)(2,1)}, bf16[128,2704]{1,0:T(8,128)(2,1)S(1)}, u32[]{:S(2)}) copy-start(bf16[128,2704]{1,0:T(8,128)(2,1)S(1)} %constant_dynamic-update-slice_fusion) | copy-start | bytes 2076676
  29.0 13.1 %collective-permute-start.9 = (bf16[48,2704]{1,0:T(8,128)(2,1)}, bf16[48,2704]{1,0:T(8,128)(2,1)S(1)}, u32[]{:S(2)}, u32[]{:S(2)}) collective-permute-start(bf16[48,2704]{1,0:T(8,128)(2,1)} %param.8), channel_id=1, source_target_pairs={{0,5},{1,4},{4,1},{5,0},{2,7},{3,6},{6,3},{7,2},{8,13},{9,12},{12,... | collective-permute-start | bytes 778760 | tf_op jit(solution)/shard_map/ppermute | solution.py:75
  42.5 0.7 copy-start.7
  43.8 1.8 %collective-permute-start.13 = (bf16[64,2652]{1,0:T(8,128)(2,1)S(1)}, bf16[64,2652]{1,0:T(8,128)(2,1)}, u32[]{:S(2)}, u32[]{:S(2)}) collective-permute-start(bf16[64,2652]{1,0:T(8,128)(2,1)S(1)} %copy.78), channel_id=1, source_target_pairs={{0,2},{2,0},{1,3},{3,1},{4,6},{6,4},{5,7},{7,5},{8,10},{10,8},{9,1... | collective-permute-start | bytes 1018376 | tf_op jit(solution)/shard_map/ppermute | solution.py:75
  43.9 14.2 %copy-start.9 = (bf16[16,2652]{1,0:T(8,128)(2,1)S(1)}, bf16[16,2652]{1,0:T(8,128)(2,1)}, u32[]{:S(2)}) copy-start(bf16[16,2652]{1,0:T(8,128)(2,1)} %param.7) | copy-start | bytes 254596
  44.3 25.9 %copy-start.8 = (f32[128,192]{0,1:T(8,128)S(1)}, f32[128,192]{0,1:T(8,128)}, u32[]{:S(2)}) copy-start(f32[128,192]{0,1:T(8,128)} %copy-done.7) | copy-start | bytes 294916
  46.7 4.6 %collective-permute-start.14 = (bf16[16,2652]{1,0:T(8,128)(2,1)S(1)}, bf16[16,2652]{1,0:T(8,128)(2,1)S(1)}, u32[]{:S(2)}, u32[]{:S(2)}) collective-permute-start(bf16[16,2652]{1,0:T(8,128)(2,1)S(1)} %get-tuple-element.31), channel_id=1, source_target_pairs={{0,8},{8,0},{16,24},{24,16},{1,9},{9,1},{17,25},{25,17},{2,10},{10... | collective-permute-start | bytes 254600 | tf_op jit(solution)/shard_map/ppermute | solution.py:75
  46.9 7.3 %collective-permute-start.16 = (bf16[16,2652]{1,0:T(8,128)(2,1)S(1)}, bf16[16,2652]{1,0:T(8,128)(2,1)S(1)}, u32[]{:S(2)}, u32[]{:S(2)}) collective-permute-start(bf16[16,2652]{1,0:T(8,128)(2,1)S(1)} %get-tuple-element.32), channel_id=1, source_target_pairs={{0,24},{8,16},{16,8},{24,0},{1,25},{9,17},{17,9},{25,1},{2,26},{10... | collective-permute-start | bytes 254600 | tf_op jit(solution)/shard_map/ppermute | solution.py:75
  47.8 10.2 %collective-permute-start.15 = (bf16[16,2652]{1,0:T(8,128)(2,1)S(1)}, bf16[16,2652]{1,0:T(8,128)(2,1)S(1)}, u32[]{:S(2)}, u32[]{:S(2)}) collective-permute-start(bf16[16,2652]{1,0:T(8,128)(2,1)S(1)} %get-tuple-element.33), channel_id=1, source_target_pairs={{0,16},{8,24},{16,0},{24,8},{1,17},{9,25},{17,1},{25,9},{2,18},{10... | collective-permute-start | bytes 254600 | tf_op jit(solution)/shard_map/ppermute | solution.py:75
  58.1 11.1 %collective-permute-start.20 = (bf16[16,2652]{1,0:T(8,128)(2,1)S(1)}, bf16[16,2652]{1,0:T(8,128)(2,1)S(1)}, u32[]{:S(2)}, u32[]{:S(2)}) collective-permute-start(bf16[16,2652]{1,0:T(8,128)(2,1)S(1)} %get-tuple-element.21), channel_id=1, source_target_pairs={{0,2},{2,0},{1,3},{3,1},{4,6},{6,4},{5,7},{7,5},{8,10},{10,8},{9,1... | collective-permute-start | bytes 254600 | tf_op jit(solution)/shard_map/ppermute | solution.py:75
  58.2 7.4 %collective-permute-start.19 = (bf16[16,2652]{1,0:T(8,128)(2,1)S(1)}, bf16[16,2652]{1,0:T(8,128)(2,1)S(1)}, u32[]{:S(2)}, u32[]{:S(2)}) collective-permute-start(bf16[16,2652]{1,0:T(8,128)(2,1)S(1)} %get-tuple-element.21), channel_id=1, source_target_pairs={{0,24},{8,16},{16,8},{24,0},{1,25},{9,17},{17,9},{25,1},{2,26},{10... | collective-permute-start | bytes 254600 | tf_op jit(solution)/shard_map/ppermute | solution.py:75
  59.5 9.2 %collective-permute-start.18 = (bf16[16,2652]{1,0:T(8,128)(2,1)S(1)}, bf16[16,2652]{1,0:T(8,128)(2,1)S(1)}, u32[]{:S(2)}, u32[]{:S(2)}) collective-permute-start(bf16[16,2652]{1,0:T(8,128)(2,1)S(1)} %get-tuple-element.21), channel_id=1, source_target_pairs={{0,16},{8,24},{16,0},{24,8},{1,17},{9,25},{17,1},{25,9},{2,18},{10... | collective-permute-start | bytes 254600 | tf_op jit(solution)/shard_map/ppermute | solution.py:75
  59.5 9.2 %collective-permute-start.17 = (bf16[16,2652]{1,0:T(8,128)(2,1)S(1)}, bf16[16,2652]{1,0:T(8,128)(2,1)S(1)}, u32[]{:S(2)}, u32[]{:S(2)}) collective-permute-start(bf16[16,2652]{1,0:T(8,128)(2,1)S(1)} %get-tuple-element.21), channel_id=1, source_target_pairs={{0,8},{8,0},{16,24},{24,16},{1,9},{9,1},{17,25},{25,17},{2,10},{10... | collective-permute-start | bytes 254600 | tf_op jit(solution)/shard_map/ppermute | solution.py:75
  65.6 4.5 %collective-permute-start.23 = (bf16[16,2652]{1,0:T(8,128)(2,1)S(1)}, bf16[16,2652]{1,0:T(8,128)(2,1)S(1)}, u32[]{:S(2)}, u32[]{:S(2)}) collective-permute-start(bf16[16,2652]{1,0:T(8,128)(2,1)S(1)} %collective-permute-done.19), channel_id=1, source_target_pairs={{0,2},{2,0},{1,3},{3,1},{4,6},{6,4},{5,7},{7,5},{8,10},{10,8},{9,1... | collective-permute-start | bytes 254600 | tf_op jit(solution)/shard_map/ppermute | solution.py:75
  68.6 1.5 %collective-permute-start.22 = (bf16[16,2652]{1,0:T(8,128)(2,1)S(1)}, bf16[16,2652]{1,0:T(8,128)(2,1)S(1)}, u32[]{:S(2)}, u32[]{:S(2)}) collective-permute-start(bf16[16,2652]{1,0:T(8,128)(2,1)S(1)} %collective-permute-done.18), channel_id=1, source_target_pairs={{0,2},{2,0},{1,3},{3,1},{4,6},{6,4},{5,7},{7,5},{8,10},{10,8},{9,1... | collective-permute-start | bytes 254600 | tf_op jit(solution)/shard_map/ppermute | solution.py:75
  68.7 1.4 %collective-permute-start.21 = (bf16[16,2652]{1,0:T(8,128)(2,1)S(1)}, bf16[16,2652]{1,0:T(8,128)(2,1)S(1)}, u32[]{:S(2)}, u32[]{:S(2)}) collective-permute-start(bf16[16,2652]{1,0:T(8,128)(2,1)S(1)} %collective-permute-done.17), channel_id=1, source_target_pairs={{0,2},{2,0},{1,3},{3,1},{4,6},{6,4},{5,7},{7,5},{8,10},{10,8},{9,1... | collective-permute-start | bytes 254600 | tf_op jit(solution)/shard_map/ppermute | solution.py:75
  74.3 17.3 %copy-start.1 = (f32[192,2652]{1,0:T(8,128)}, f32[192,2652]{1,0:T(8,128)S(1)}, u32[]{:S(2)}) copy-start(f32[192,2652]{1,0:T(8,128)S(1)} %get-tuple-element.43) | copy-start | bytes 6110212
  74.3 27.0 %copy-start = (f32[192,2704]{1,0:T(8,128)S(1)}, f32[192,2704]{1,0:T(8,128)}, u32[]{:S(2)}) copy-start(f32[192,2704]{1,0:T(8,128)} %get-tuple-element.41) | copy-start | bytes 6230020
  74.4 14.7 %collective-permute-start.27 = (bf16[48,2652]{1,0:T(8,128)(2,1)S(1)}, bf16[48,2652]{1,0:T(8,128)(2,1)S(1)}, u32[]{:S(2)}, u32[]{:S(2)}) collective-permute-start(bf16[48,2652]{1,0:T(8,128)(2,1)S(1)} %get-tuple-element.28), channel_id=1, source_target_pairs={{0,1},{1,0},{4,5},{5,4},{2,3},{3,2},{6,7},{7,6},{8,9},{9,8},{12,13... | collective-permute-start | bytes 763784 | tf_op jit(solution)/shard_map/ppermute | solution.py:75
  76.0 14.8 %collective-permute-start.29 = (bf16[48,2652]{1,0:T(8,128)(2,1)S(1)}, bf16[48,2652]{1,0:T(8,128)(2,1)S(1)}, u32[]{:S(2)}, u32[]{:S(2)}) collective-permute-start(bf16[48,2652]{1,0:T(8,128)(2,1)S(1)} %get-tuple-element.29), channel_id=1, source_target_pairs={{0,5},{1,4},{4,1},{5,0},{2,7},{3,6},{6,3},{7,2},{8,13},{9,12},{12,... | collective-permute-start | bytes 763784 | tf_op jit(solution)/shard_map/ppermute | solution.py:75
  77.0 13.8 %collective-permute-start.28 = (bf16[48,2652]{1,0:T(8,128)(2,1)S(1)}, bf16[48,2652]{1,0:T(8,128)(2,1)S(1)}, u32[]{:S(2)}, u32[]{:S(2)}) collective-permute-start(bf16[48,2652]{1,0:T(8,128)(2,1)S(1)} %get-tuple-element.30), channel_id=1, source_target_pairs={{0,4},{1,5},{4,0},{5,1},{2,6},{3,7},{6,2},{7,3},{8,12},{9,13},{12,... | collective-permute-start | bytes 763784 | tf_op jit(solution)/shard_map/ppermute | solution.py:75
  78.0 22.1 %collective-permute-start.24 = (bf16[48,2704]{1,0:T(8,128)(2,1)S(1)}, bf16[48,2704]{1,0:T(8,128)(2,1)S(1)}, u32[]{:S(2)}, u32[]{:S(2)}) collective-permute-start(bf16[48,2704]{1,0:T(8,128)(2,1)S(1)} %get-tuple-element.25), channel_id=1, source_target_pairs={{0,1},{1,0},{4,5},{5,4},{2,3},{3,2},{6,7},{7,6},{8,9},{9,8},{12,13... | collective-permute-start | bytes 778760 | tf_op jit(solution)/shard_map/ppermute | solution.py:75
  79.6 20.5 %collective-permute-start.26 = (bf16[48,2704]{1,0:T(8,128)(2,1)S(1)}, bf16[48,2704]{1,0:T(8,128)(2,1)S(1)}, u32[]{:S(2)}, u32[]{:S(2)}) collective-permute-start(bf16[48,2704]{1,0:T(8,128)(2,1)S(1)} %get-tuple-element.26), channel_id=1, source_target_pairs={{0,5},{1,4},{4,1},{5,0},{2,7},{3,6},{6,3},{7,2},{8,13},{9,12},{12,... | collective-permute-start | bytes 778760 | tf_op jit(solution)/shard_map/ppermute | solution.py:75
  89.1 12.3 %collective-permute-start.25 = (bf16[48,2704]{1,0:T(8,128)(2,1)S(1)}, bf16[48,2704]{1,0:T(8,128)(2,1)S(1)}, u32[]{:S(2)}, u32[]{:S(2)}) collective-permute-start(bf16[48,2704]{1,0:T(8,128)(2,1)S(1)} %get-tuple-element.27), channel_id=1, source_target_pairs={{0,4},{1,5},{4,0},{5,1},{2,6},{3,7},{6,2},{7,3},{8,12},{9,13},{12,... | collective-permute-start | bytes 778760 | tf_op jit(solution)/shard_map/ppermute | solution.py:75
  90.8 10.5 %copy-start.2 = (bf16[48,2652]{1,0:T(8,128)(2,1)}, bf16[48,2652]{1,0:T(8,128)(2,1)S(1)}, u32[]{:S(2)}) copy-start(bf16[48,2652]{1,0:T(8,128)(2,1)S(1)} %collective-permute-done.29) | copy-start | bytes 763780
  90.8 10.5 %copy-start.4 = (bf16[48,2652]{1,0:T(8,128)(2,1)}, bf16[48,2652]{1,0:T(8,128)(2,1)S(1)}, u32[]{:S(2)}) copy-start(bf16[48,2652]{1,0:T(8,128)(2,1)S(1)} %collective-permute-done.28) | copy-start | bytes 763780
  101.4 15.0 %copy-start.3 = (bf16[48,2652]{1,0:T(8,128)(2,1)S(1)}, bf16[48,2652]{1,0:T(8,128)(2,1)}, u32[]{:S(2)}) copy-start(bf16[48,2652]{1,0:T(8,128)(2,1)} %copy-done.2) | copy-start | bytes 763780
  113.5 2.9 %copy-start.5 = (bf16[48,2652]{1,0:T(8,128)(2,1)S(1)}, bf16[48,2652]{1,0:T(8,128)(2,1)}, u32[]{:S(2)}) copy-start(bf16[48,2652]{1,0:T(8,128)(2,1)} %copy-done.4) | copy-start | bytes 763780
